TPU v7x, 32 devices: a whole 2x2x4 slice. The times are simulated.
32 devices in a mesh: gx: 16 (over z, y, x), gy: 2 (over core).
Axes of the slice: x: 2, y: 2, z: 4, core: 2. Of those that a mesh axis runs over, the one named last changes fastest.
Arguments:
- history: bfloat16 [128, 2048, 256], P(('gx', 'gy')), may hold values from -100 to 100
- lengths: int32 [128], P(('gx', 'gy')), may hold values from 16 to 2048
- candidates: int32 [128, 64], P(('gx', 'gy')), may hold values from 0 to 131071, as said below
- item_table: bfloat16 [131072, 512], P(('gx', 'gy')), may hold values from -6 to 6
- value_weight: bfloat16 [256, 256], replicated, may hold values from -0.375 to 0.375
- click_hidden: bfloat16 [768, 256], replicated, may hold values from -0.21875 to 0.21875
- convert_hidden: bfloat16 [768, 256], replicated, may hold values from -0.21875 to 0.21875
- click_output: bfloat16 [256], replicated, may hold values from -0.75 to 0.75
- convert_output: bfloat16 [256], replicated, may hold values from -0.75 to 0.75
Outputs:
- click_rate: float32 [128, 64], P(('gx', 'gy'))
- click_conversion: float32 [128, 64], P(('gx', 'gy'))
Inputs may be any that keep to these rules, and one draw needn't show every extreme that they name: Device k holds the table rows k * 4096 to (k + 1) * 4096 - 1. Of the 256 candidates of one device, at most 16 are items of one device's rows, and exactly 16 are items of some device's rows.
All inputs are finite; a program needn't handle non-finite values.
Results may differ from a plain program's by a relative error of at most 0.0028.
Values may be sent and summed in bfloat16 or wider, within the bound.
A program may use at most 64 MiB of HBM per device.

v0:
```python
import functools
import math

import jax
import jax.numpy as jnp
from jax import lax
from jax.experimental import pallas as pl
from jax.experimental.pallas import tpu as pltpu
from jax.sharding import PartitionSpec as P

HEADS = 4
CHUNK = 512
SPLIT = 256
MESH = pl.DeviceIdType.MESH
neg_big = -1e30
f32, bf16 = jnp.float32, jnp.bfloat16


def dot(a, b, dims=((1,), (0,))):
    return lax.dot_general(a, b, (dims, ((), ())), preferred_element_type=f32)


def iota(shape, axis):
    return lax.broadcasted_iota(jnp.int32, shape, axis)


def exchange_kernel(
    n,
    ny,
    cap,
    cand_ref,
    table_hbm,
    out_ref,
    table,
    id_send,
    id_recv,
    slabs,
    rows_recv,
    sems,
):
    me = lax.axis_index("gx") * ny + lax.axis_index("gy")
    users, per_user = cand_ref.shape
    total = users * per_user
    table_rows = table.shape[0]

    load = pltpu.make_async_copy(table_hbm, table, sems.at[4])
    load.start()

    def at(j):
        d = lax.rem(me + j, n)
        return d, (lax.div(d, ny), lax.rem(d, ny))

    barrier = pltpu.get_barrier_semaphore()

    def greet(j, c):
        pl.semaphore_signal(barrier, inc=1, device_id=at(j)[1], device_id_type=MESH)
        return c

    lax.fori_loop(1, n, greet, 0)

    ids = jnp.concatenate([cand_ref[u : u + 1, :] for u in range(users)], axis=1)
    first = iota((n, total), 0) * table_rows
    local = ids - first
    mine = (local >= 0) & (local < table_rows)
    hot = jnp.where(mine, 1.0, 0.0).astype(f32)
    earlier = jnp.where(iota((total, total), 0) < iota((total, total), 1), 1.0, 0.0).astype(bf16)
    rank = jnp.sum(hot * dot(hot.astype(bf16), earlier), axis=0, keepdims=True)
    owner = jnp.sum(hot * iota((n, total), 0).astype(f32), axis=0, keepdims=True)
    slot = (owner * cap + rank).astype(jnp.int32)
    high = jnp.where(mine, local // SPLIT, 0).astype(f32).astype(bf16)
    low = jnp.where(mine, local % SPLIT, 0).astype(f32).astype(bf16)
    rank_i = rank.astype(jnp.int32)
    lane = iota((128, total), 0)
    at_high = jnp.where(lane == rank_i, 1.0, 0.0).astype(bf16)
    at_low = jnp.where(lane == rank_i + cap, 1.0, 0.0).astype(bf16)
    request = dot(high, at_high, ((1,), (1,))) + dot(low, at_low, ((1,), (1,)))
    for d in range(n):
        id_send[d] = request[d : d + 1, :]

    pl.semaphore_wait(barrier, n - 1)

    def ask(j, c):
        d, where = at(j)
        pltpu.make_async_remote_copy(
            src_ref=id_send.at[d],
            dst_ref=id_recv.at[me],
            send_sem=sems.at[0],
            recv_sem=sems.at[1],
            device_id=where,
            device_id_type=MESH,
        ).start()
        return c

    lax.fori_loop(1, n, ask, 0)
    id_recv[me] = id_send[me]

    same = iota((total, total), 0) == iota((total, total), 1)
    slot_col = jnp.sum(jnp.where(same, slot.astype(f32), 0.0), axis=1, keepdims=True)
    slot_col = slot_col.astype(jnp.int32)

    others = pl.ds(0, n - 1)

    def drain(ref, sem):
        pltpu.make_async_copy(ref.at[others], ref.at[others], sem).wait()

    load.wait()
    drain(id_recv, sems.at[1])

    group = 256 // cap
    asked = jnp.concatenate([id_recv[d] for d in range(n)], axis=0).astype(bf16)
    for g in range(n // group):
        base = g * group
        row = iota((256, n), 0)
        source = lax.rem(me + base + row // cap, n)
        expand = jnp.where(source == iota((256, n), 1), 1.0, 0.0).astype(bf16)
        spread = dot(expand, asked)
        place = iota((256, 128), 0) % cap
        lane = iota((256, 128), 1)
        weight = jnp.where(lane == place, float(SPLIT), jnp.where(lane == place + cap, 1.0, 0.0))
        wanted = jnp.sum(spread * weight, axis=1, keepdims=True).astype(jnp.int32)
        pick = jnp.where(wanted == iota((256, table_rows), 1), 1.0, 0.0).astype(bf16)
        found = dot(pick, table[...]).astype(bf16)
        for k in range(group):
            slabs[base + k] = found[k * cap : (k + 1) * cap, :]

        def answer(j, c):
            _, where = at(j)
            pltpu.make_async_remote_copy(
                src_ref=slabs.at[j],
                dst_ref=rows_recv.at[me],
                send_sem=sems.at[2],
                recv_sem=sems.at[3],
                device_id=where,
                device_id_type=MESH,
            ).start()
            return c

        lax.fori_loop(max(base, 1), base + group, answer, 0)
    rows_recv[me] = slabs[0]
    choose = jnp.where(slot_col == iota((total, n * cap), 1), 1.0, 0.0).astype(bf16)
    drain(rows_recv, sems.at[3])
    arrived = rows_recv[...].reshape(n * cap, rows_recv.shape[2])
    out_ref[...] = dot(choose, arrived).astype(bf16)
    drain(id_send, sems.at[0])
    drain(slabs, sems.at[2])


def exchange(candidates, item_table, n, ny):
    users, per_user = candidates.shape
    total = users * per_user
    table_rows, width = item_table.shape
    cap = max(2 * total // n, 16)
    return pl.pallas_call(
        functools.partial(exchange_kernel, n, ny, cap),
        out_shape=jax.ShapeDtypeStruct((total, width), bf16),
        in_specs=[
            pl.BlockSpec(memory_space=pltpu.VMEM),
            pl.BlockSpec(memory_space=pl.ANY),
        ],
        out_specs=pl.BlockSpec(memory_space=pltpu.VMEM),
        scratch_shapes=[
            pltpu.VMEM((table_rows, width), bf16),
            pltpu.VMEM((n, 1, 128), f32),
            pltpu.VMEM((n, 1, 128), f32),
            pltpu.VMEM((n, cap, width), bf16),
            pltpu.VMEM((n, cap, width), bf16),
            pltpu.SemaphoreType.DMA((5,)),
        ],
        compiler_params=pltpu.CompilerParams(collective_id=0, has_side_effects=True),
        name="exchange",
    )(candidates, item_table)


def attend_kernel(
    len_ref,
    hist_hbm,
    rows_ref,
    value_ref,
    click_ref,
    convert_ref,
    click_out_ref,
    convert_out_ref,
    rate_ref,
    both_ref,
    hist,
    joined,
    top_ref,
    sum_ref,
    ctx_ref,
    sems,
):
    users, seq, width = hist.shape
    per_user = rate_ref.shape[1]
    head = width // HEADS
    queries = HEADS * per_user
    chunks = seq // CHUNK
    scale = math.log2(math.e) / math.sqrt(head)

    def piece(u, c):
        rows = pl.ds(c * CHUNK, CHUNK)
        return pltpu.make_async_copy(hist_hbm.at[u, rows], hist.at[u, rows], sems.at[u, c])

    count = [(len_ref[u] + CHUNK - 1) // CHUNK for u in range(users)]
    for u in range(users):
        for c in range(chunks):

            @pl.when(c < count[u])
            def _():
                piece(u, c).start()

    lane_head = iota((per_user, width), 1) // head
    for u in range(users):
        mine = pl.ds(u * per_user, per_user)
        target = rows_ref[mine, :width]
        query = jnp.concatenate(
            [jnp.where(lane_head == h, target, jnp.zeros_like(target)) for h in range(HEADS)], axis=0
        )
        top_ref[...] = jnp.full(top_ref.shape, neg_big, f32)
        sum_ref[...] = jnp.zeros(sum_ref.shape, f32)
        ctx_ref[...] = jnp.zeros(ctx_ref.shape, f32)
        length = len_ref[u]

        def turn(c, carry):
            piece(u, c).wait()
            block = hist[u, pl.ds(pl.multiple_of(c * CHUNK, CHUNK), CHUNK), :]
            score = dot(query, block, ((1,), (1,))) * scale
            live = iota((queries, CHUNK), 1) < length - c * CHUNK
            score = jnp.where(live, score, neg_big)
            old = top_ref[...]
            new = jnp.maximum(old, jnp.max(score, axis=1, keepdims=True))
            weight = jnp.exp2(score - new).astype(bf16)
            keep = jnp.exp2(old - new)
            top_ref[...] = new
            sum_ref[...] = sum_ref[...] * keep + jnp.sum(weight.astype(f32), axis=1, keepdims=True)
            ctx_ref[...] = ctx_ref[...] * keep + dot(weight, block)
            return carry

        lax.fori_loop(0, count[u], turn, 0)
        context = ctx_ref[...]
        part0 = context.astype(bf16)
        rest = context - part0.astype(f32)
        part1 = rest.astype(bf16)
        part2 = (rest - part1.astype(f32)).astype(bf16)
        value = value_ref[...]
        full = (dot(part0, value) + dot(part1, value) + dot(part2, value)) / sum_ref[...]
        pooled = jnp.zeros((per_user, width), f32)
        for h in range(HEADS):
            pooled = jnp.where(lane_head == h, full[h * per_user : (h + 1) * per_user, :], pooled)
        normed = pooled * lax.rsqrt(jnp.mean(pooled * pooled, axis=1, keepdims=True) + 1e-6)
        joined[mine, :width] = normed.astype(bf16)
    joined[:, width:] = rows_ref[...]
    every = joined[...]

    def tower(hidden_ref, output_ref):
        act = jnp.maximum(dot(every, hidden_ref[...]), 0.0).astype(bf16)
        return 1.0 / (1.0 + jnp.exp(-dot(output_ref[...], act, ((1,), (1,)))))

    rate = tower(click_ref, click_out_ref)
    both = rate * tower(convert_ref, convert_out_ref)
    for u in range(users):
        mine = slice(u * per_user, (u + 1) * per_user)
        rate_ref[u : u + 1, :] = rate[:, mine]
        both_ref[u : u + 1, :] = both[:, mine]


def attend(history, lengths, rows, value, click, convert, click_out, convert_out, per_user):
    users, seq, width = history.shape
    queries = HEADS * per_user
    vmem = pl.BlockSpec(memory_space=pltpu.VMEM)
    out = jax.ShapeDtypeStruct((users, per_user), f32)
    return pl.pallas_call(
        attend_kernel,
        out_shape=(out, out),
        in_specs=[
            pl.BlockSpec(memory_space=pltpu.SMEM),
            pl.BlockSpec(memory_space=pl.ANY),
        ]
        + [vmem] * 6,
        out_specs=(vmem, vmem),
        scratch_shapes=[
            pltpu.VMEM((users, seq, width), bf16),
            pltpu.VMEM((users * per_user, 3 * width), bf16),
            pltpu.VMEM((queries, 1), f32),
            pltpu.VMEM((queries, 1), f32),
            pltpu.VMEM((queries, width), f32),
            pltpu.SemaphoreType.DMA((users, seq // CHUNK)),
        ],
        name="attend",
    )(lengths, history, rows, value, click, convert, click_out, convert_out)


def local(
    n,
    ny,
    history,
    lengths,
    candidates,
    item_table,
    value_weight,
    click_hidden,
    convert_hidden,
    click_output,
    convert_output,
):
    rows = exchange(candidates, item_table, n, ny)
    return attend(
        history,
        lengths,
        rows,
        value_weight,
        click_hidden,
        convert_hidden,
        click_output.reshape(1, -1),
        convert_output.reshape(1, -1),
        candidates.shape[1],
    )


def solution(mesh):
    both = ("gx", "gy")
    placed = (P(both, None, None), P(both), P(both, None), P(both, None), P(), P(), P(), P(), P())
    return jax.shard_map(
        functools.partial(local, mesh.shape["gx"] * mesh.shape["gy"], mesh.shape["gy"]),
        mesh=mesh,
        in_specs=placed,
        out_specs=(P(both, None), P(both, None)),
        check_vma=False,
    )
```

profile of v0, /device:TPU:12, one launch (start us, length us, event | category | flops | bytes accessed | tf_op | source)
XLA Modules:
  0.0 42.1 jit_solution(9451848763283229667)
XLA Ops:
  0.6 1.2 %reshape.10.click_out_ref = bf16[1,256]{1,0:T(2,128)(2,1)} reshape(bf16[256]{0:T(256)(128)(2,1)} %param.16) | data formatting | bytes 1024 | tf_op jit(solution)/shard_map/reshape | solution.py:313
  1.9 1.2 %reshape.11.convert_out_ref = bf16[1,256]{1,0:T(2,128)(2,1)} reshape(bf16[256]{0:T(256)(128)(2,1)} %param.17) | data formatting | bytes 1024 | tf_op jit(solution)/shard_map/reshape | solution.py:314
  3.1 24.8 %exchange.1.rows_ref = bf16[256,512]{1,0:T(8,128)(2,1)} custom-call(s32[4,64]{1,0:T(4,128)} %cand_ref.1, bf16[4096,512]{1,0:T(8,128)(2,1)} %table_hbm.1), custom_call_target="tpu_custom_call" | custom-call | tf_op jit(solution)/shard_map/exchange/pallas_call | solution.py:153
  27.9 14.2 %attend.1 = (f32[4,64]{1,0:T(4,128)}, f32[4,64]{1,0:T(4,128)}) custom-call(s32[4]{0:T(128)} %len_ref.1, bf16[4,2048,256]{2,1,0:T(8,128)(2,1)} %hist_hbm.1, bf16[256,512]{1,0:T(8,128)(2,1)} %exchange.1.rows_ref, bf16[256,256]{1,0:T(8,128)(2,1)} %value_ref.1, bf16[768,256]{1,0:T(8,128)(2,1)} %click_ref.1, bf16[768,256]{1,0:T(8,128)(2,1)} %convert_ref.1, ...), custom_call_target="tpu_custom_call" | custom-call | tf_op jit(solution)/shard_map/attend/pallas_call | solution.py:271
where the time goes:
time: 42.3 us; the launch traced here: 42.1 us
  Pallas kernels  39 us (92%)
  local copies, waits for them, and re-layouts  2.47 us (6%)
  between operations  0.64 us (2%)
    pallas_call x1, Pallas kernels, exchange(): pl.pallas_call(functools.partial(exchange_kernel, n, ny, cap), out_shape=...  24.8 us
    pallas_call x1, Pallas kernels, attend(): pl.pallas_call(attend_kernel, out_shape=(out, out), in_specs=[pl.BlockSpe...  14.2 us
    reshape x1, local copies, waits for them, and re-layouts, local(): convert_output.reshape(1, -1)  1.24 us
    reshape x1, local copies, waits for them, and re-layouts, local(): click_output.reshape(1, -1)  1.23 us

commit v1 on v0

v1 whole, which is shorter than its diff:
```python
import functools
import math

import jax
import jax.numpy as jnp
from jax import lax
from jax.experimental import pallas as pl
from jax.experimental.pallas import tpu as pltpu
from jax.sharding import PartitionSpec as P

HEADS = 4
CHUNK = 512
SPLIT = 256
MESH = pl.DeviceIdType.MESH
neg_big = -1e30
f32, bf16 = jnp.float32, jnp.bfloat16


def dot(a, b, dims=((1,), (0,))):
    return lax.dot_general(a, b, (dims, ((), ())), preferred_element_type=f32)


def iota(shape, axis):
    return lax.broadcasted_iota(jnp.int32, shape, axis)


def fused_kernel(
    n,
    ny,
    cap,
    len_ref,
    cand_ref,
    click_out_ref,
    convert_out_ref,
    table_hbm,
    hist_hbm,
    value_hbm,
    click_hbm,
    convert_hbm,
    rate_ref,
    both_ref,
    table,
    hist,
    value,
    click,
    convert,
    id_send,
    id_recv,
    pick,
    target_send,
    target_recv,
    feature_send,
    feature_recv,
    scores,
    tops,
    joined,
    load_sems,
    sems,
):
    me = lax.axis_index("gx") * ny + lax.axis_index("gy")
    users, per_user = cand_ref.shape
    seq, width = hist.shape[1:]
    total = users * per_user
    table_rows = table.shape[0]

    loads = [
        pltpu.make_async_copy(src, dst, load_sems.at[i])
        for i, (src, dst) in enumerate(
            [(table_hbm, table), (value_hbm, value), (click_hbm, click), (convert_hbm, convert)]
            + [(hist_hbm.at[u], hist.at[u]) for u in range(users)]
        )
    ]
    loads[0].start()

    def at(j):
        d = lax.rem(me + j, n)
        return d, (lax.div(d, ny), lax.rem(d, ny))

    barrier = pltpu.get_barrier_semaphore()

    def greet(j, c):
        pl.semaphore_signal(barrier, inc=1, device_id=at(j)[1], device_id_type=MESH)
        return c

    lax.fori_loop(1, n, greet, 0)
    for load in loads[4:] + loads[1:4]:
        load.start()

    ids = jnp.concatenate([cand_ref[u : u + 1, :] for u in range(users)], axis=1)
    first = iota((n, total), 0) * table_rows
    local = ids - first
    mine = (local >= 0) & (local < table_rows)
    hot = jnp.where(mine, 1.0, 0.0).astype(f32)
    earlier = jnp.where(iota((total, total), 0) < iota((total, total), 1), 1.0, 0.0).astype(bf16)
    rank = jnp.sum(hot * dot(hot.astype(bf16), earlier), axis=0, keepdims=True)
    owner = jnp.sum(hot * iota((n, total), 0).astype(f32), axis=0, keepdims=True)
    slot = owner * cap + rank
    high = jnp.where(mine, local // SPLIT, 0).astype(f32).astype(bf16)
    low = jnp.where(mine, local % SPLIT, 0).astype(f32).astype(bf16)
    rank_i = rank.astype(jnp.int32)
    lane = iota((128, total), 0)
    at_high = jnp.where(lane == rank_i, 1.0, 0.0).astype(bf16)
    at_low = jnp.where(lane == rank_i + cap, 1.0, 0.0).astype(bf16)
    request = dot(high, at_high, ((1,), (1,))) + dot(low, at_low, ((1,), (1,)))
    for d in range(n):
        id_send[d] = request[d : d + 1, :]

    def send(src, dst, lo, hi, sem, by_owner):
        def one(j, c):
            d, where = at(j)
            pltpu.make_async_remote_copy(
                src_ref=src.at[d if by_owner else j],
                dst_ref=dst.at[me],
                send_sem=sems.at[sem],
                recv_sem=sems.at[sem + 1],
                device_id=where,
                device_id_type=MESH,
            ).start()
            return c

        lax.fori_loop(max(lo, 1), hi, one, 0)

    others = pl.ds(0, n - 1)

    def drain(ref, sem):
        pltpu.make_async_copy(ref.at[others], ref.at[others], sems.at[sem]).wait()

    pl.semaphore_wait(barrier, n - 1)
    send(id_send, id_recv, 1, n, 0, True)
    id_recv[me] = id_send[me]

    same = iota((total, total), 0) == iota((total, total), 1)
    slot_col = jnp.sum(jnp.where(same, slot, 0.0), axis=1, keepdims=True).astype(jnp.int32)
    choose = jnp.where(slot_col == iota((total, n * cap), 1), 1.0, 0.0).astype(bf16)

    drain(id_recv, 1)
    group = 256 // cap
    asked = jnp.concatenate([id_recv[d] for d in range(n)], axis=0).astype(bf16)
    loads[0].wait()
    for g in range(n // group):
        base = g * group
        source = lax.rem(me + base + iota((256, n), 0) // cap, n)
        expand = jnp.where(source == iota((256, n), 1), 1.0, 0.0).astype(bf16)
        spread = dot(expand, asked)
        place = iota((256, 128), 0) % cap
        lane = iota((256, 128), 1)
        weight = jnp.where(lane == place, float(SPLIT), jnp.where(lane == place + cap, 1.0, 0.0))
        wanted = jnp.sum(spread * weight, axis=1, keepdims=True).astype(jnp.int32)
        pick[g] = jnp.where(wanted == iota((256, table_rows), 1), 1.0, 0.0).astype(bf16)
        found = dot(pick[g], table[:, :width]).astype(bf16)
        for k in range(group):
            target_send[base + k] = found[k * cap : (k + 1) * cap, :]
        send(target_send, target_recv, base, base + group, 2, False)
    for g in range(n // group):
        base = g * group
        found = dot(pick[g], table[:, width:]).astype(bf16)
        for k in range(group):
            feature_send[base + k] = found[k * cap : (k + 1) * cap, :]
        send(feature_send, feature_recv, base, base + group, 4, False)
    target_recv[me] = target_send[0]
    feature_recv[me] = feature_send[0]

    for load in loads[1:]:
        load.wait()
    drain(target_recv, 3)
    target = dot(choose, target_recv[...].reshape(n * cap, width)).astype(bf16)
    joined[:, width : 2 * width] = target

    head = width // HEADS
    queries = HEADS * per_user
    scale = math.log2(math.e) / math.sqrt(head)
    lane_head = iota((per_user, width), 1) // head
    chunks = seq // CHUNK
    slabs = CHUNK // 128

    def query_of(u):
        own = target[u * per_user : (u + 1) * per_user, :]
        return jnp.concatenate(
            [jnp.where(lane_head == h, own, jnp.zeros_like(own)) for h in range(HEADS)], axis=0
        )

    def score(u, c, query, top):
        s = dot(query, hist[u, c * CHUNK : (c + 1) * CHUNK, :], ((1,), (1,))) * scale
        live = iota((queries, CHUNK), 1) < len_ref[u] - c * CHUNK
        s = jnp.where(live, s, neg_big)
        scores[u % 2, :, c * CHUNK : (c + 1) * CHUNK] = s
        for k in range(slabs):
            part = s[:, k * 128 : (k + 1) * 128]
            top = part if top is None else jnp.maximum(top, part)
        return top

    def finish(u, top):
        tops[u % 2] = jnp.broadcast_to(jnp.max(top, axis=1, keepdims=True), (queries, 128))

    def gather(u, c, total_weight, context):
        top = tops[u % 2]
        parts = []
        for k in range(slabs):
            at_k = c * CHUNK + k * 128
            w = jnp.exp2(scores[u % 2, :, at_k : at_k + 128] - top).astype(bf16)
            wide = w.astype(f32)
            total_weight = wide if total_weight is None else total_weight + wide
            parts.append(w)
        more = dot(jnp.concatenate(parts, axis=1), hist[u, c * CHUNK : (c + 1) * CHUNK, :])
        return total_weight, more if context is None else context + more

    def interest(u, total_weight, context):
        part0 = context.astype(bf16)
        rest = context - part0.astype(f32)
        part1 = rest.astype(bf16)
        part2 = (rest - part1.astype(f32)).astype(bf16)
        full = dot(part0, value[...]) + dot(part1, value[...]) + dot(part2, value[...])
        full = full / jnp.sum(total_weight, axis=1, keepdims=True)
        pooled = jnp.zeros((per_user, width), f32)
        for h in range(HEADS):
            pooled = jnp.where(lane_head == h, full[h * per_user : (h + 1) * per_user, :], pooled)
        normed = pooled * lax.rsqrt(jnp.mean(pooled * pooled, axis=1, keepdims=True) + 1e-6)
        joined[u * per_user : (u + 1) * per_user, :width] = normed.astype(bf16)

    query = query_of(0)
    top = None
    for c in range(chunks):
        top = score(0, c, query, top)
    finish(0, top)
    for u in range(users):
        if u + 1 < users:
            query = query_of(u + 1)
        top = total_weight = context = None
        for c in range(chunks):
            if u + 1 < users:
                top = score(u + 1, c, query, top)
            total_weight, context = gather(u, c, total_weight, context)
        if u + 1 < users:
            finish(u + 1, top)
        interest(u, total_weight, context)

    drain(feature_recv, 5)
    feature = dot(choose, feature_recv[...].reshape(n * cap, width))
    joined[:, 2 * width :] = feature.astype(bf16)
    every = joined[...]

    def tower(hidden, output_ref):
        act = jnp.maximum(dot(every, hidden[...]), 0.0).astype(bf16)
        last = output_ref[...].reshape(1, -1)
        return 1.0 / (1.0 + jnp.exp(-dot(last, act, ((1,), (1,)))))

    rate = tower(click, click_out_ref)
    both = rate * tower(convert, convert_out_ref)
    for u in range(users):
        own = slice(u * per_user, (u + 1) * per_user)
        rate_ref[u : u + 1, :] = rate[:, own]
        both_ref[u : u + 1, :] = both[:, own]
    drain(id_send, 0)
    drain(target_send, 2)
    drain(feature_send, 4)


def local(
    n,
    ny,
    history,
    lengths,
    candidates,
    item_table,
    value_weight,
    click_hidden,
    convert_hidden,
    click_output,
    convert_output,
):
    users, per_user = candidates.shape
    seq, width = history.shape[1:]
    total = users * per_user
    cap = max(2 * total // n, 16)
    queries = HEADS * per_user
    vmem = pl.BlockSpec(memory_space=pltpu.VMEM)
    hbm = pl.BlockSpec(memory_space=pl.ANY)
    out = jax.ShapeDtypeStruct((users, per_user), f32)
    slab = pltpu.VMEM((n, cap, width), bf16)
    held = [item_table, history, value_weight, click_hidden, convert_hidden]
    return pl.pallas_call(
        functools.partial(fused_kernel, n, ny, cap),
        out_shape=(out, out),
        in_specs=[pl.BlockSpec(memory_space=pltpu.SMEM)] + [vmem] * 3 + [hbm] * 5,
        out_specs=(vmem, vmem),
        scratch_shapes=[pltpu.VMEM(x.shape, x.dtype) for x in held]
        + [
            pltpu.VMEM((n, 1, 128), f32),
            pltpu.VMEM((n, 1, 128), f32),
            pltpu.VMEM((n * cap // 256, 256, item_table.shape[0]), bf16),
            slab,
            slab,
            slab,
            slab,
            pltpu.VMEM((2, queries, seq), f32),
            pltpu.VMEM((2, queries, 128), f32),
            pltpu.VMEM((total, 3 * width), bf16),
            pltpu.SemaphoreType.DMA((4 + users,)),
            pltpu.SemaphoreType.DMA((6,)),
        ],
        compiler_params=pltpu.CompilerParams(collective_id=0, has_side_effects=True),
        name="esmm",
    )(lengths, candidates, click_output, convert_output, *held)


def solution(mesh):
    both = ("gx", "gy")
    placed = (P(both, None, None), P(both), P(both, None), P(both, None), P(), P(), P(), P(), P())
    return jax.shard_map(
        functools.partial(local, mesh.shape["gx"] * mesh.shape["gy"], mesh.shape["gy"]),
        mesh=mesh,
        in_specs=placed,
        out_specs=(P(both, None), P(both, None)),
        check_vma=False,
    )
```

time: 42.3 us -> 32.5 us (0.77)
  Pallas kernels: 39 us -> 28.9 us
    pallas_call x2 -> x1, Pallas kernels: 39 us -> 28.9 us  [local(): pl.pallas_call(functools.partial(fused_kernel, n, ny, cap), out_shape=(ou...]
    unnamed x0 -> x2, local copies, waits for them, and re-layouts: none -> 2.48 us
    reshape x2 -> x0, local copies, waits for them, and re-layouts: 2.47 us -> none  [the longest x1 1.24 us: local(): convert_output.reshape(1, -1)]
where the time goes in v1:
time: 32.5 us; the launch traced here: 32 us
  Pallas kernels  28.9 us (89%)
  local copies, waits for them, and re-layouts  2.48 us (8%)
  between operations  0.64 us (2%)
    pallas_call x1, Pallas kernels, local(): pl.pallas_call(functools.partial(fused_kernel, n, ny, cap), out_shape=(ou...  28.9 us
    unnamed x2, local copies, waits for them, and re-layouts  2.48 us

profile of v1, /device:TPU:12, one launch (start us, length us, event | category | flops | bytes accessed | tf_op | source)
XLA Modules:
  0.0 32.0 jit_solution(1595389926566344167)
XLA Ops:
  0.6 28.9 %esmm.1 = (f32[4,64]{1,0:T(4,128)}, f32[4,64]{1,0:T(4,128)}) custom-call(s32[4]{0:T(128)} %len_ref.1, s32[4,64]{1,0:T(4,128)} %cand_ref.1, bf16[256]{0:T(256)(128)(2,1)} %click_out_ref.1, bf16[256]{0:T(256)(128)(2,1)} %convert_out_ref.1, bf16[4096,512]{1,0:T(8,128)(2,1)} %table_hbm.1, bf16[4,2048,256]{2,1,0:T(8,128)(2,1)} %hist_hbm.1, ...), custom_call_target="tpu_custom_call" | custom-call | tf_op jit(solution)/shard_map/esmm/pallas_call | solution.py:281
  29.5 1.2 %copy.13 = f32[4,64]{1,0:T(4,128)} copy(f32[4,64]{1,0:T(4,128)} %get-tuple-element.4) | data formatting | bytes 2048
  30.8 1.2 %copy.14 = f32[4,64]{1,0:T(4,128)} copy(f32[4,64]{1,0:T(4,128)} %get-tuple-element.5) | data formatting | bytes 2048

commit v2 on v1

--- a/solution.py
+++ b/solution.py
@@ -37,8 +37,7 @@
     value_hbm,
     click_hbm,
     convert_hbm,
-    rate_ref,
-    both_ref,
+    logit_ref,
     table,
     hist,
     value,
@@ -72,17 +71,41 @@
     ]
     loads[0].start()
 
-    def at(j):
-        d = lax.rem(me + j, n)
-        return d, (lax.div(d, ny), lax.rem(d, ny))
+    half = n // ny // 2
+    gx, gy = lax.axis_index("gx"), lax.axis_index("gy")
+    upper = jnp.where(gx >= half, 1, 0)
+    inner = gx - upper * half
+
+    def walk(lo, hi, act):
+        far = lo < n // 2
+        skip = 0 if far else half
+        start = (1 - upper if far else upper) * half
+
+        def visit(a, b):
+            x = inner + (a - skip)
+            x = start + jnp.where(x >= half, x - half, x)
+            y = gy + b
+            y = jnp.where(y >= ny, y - ny, y)
+            act(a * ny + b, x * ny + y, (x, y))
+
+        def step(a, c):
+            for b in range(ny):
+                visit(a, b)
+            return c
+
+        first = lo // ny
+        if lo == n // 2:
+            for b in range(1, ny):
+                visit(first, b)
+            first += 1
+        lax.fori_loop(first, hi // ny, step, 0)
+
+    def greet(j, d, where):
+        pl.semaphore_signal(barrier, inc=1, device_id=where, device_id_type=MESH)
 
     barrier = pltpu.get_barrier_semaphore()
-
-    def greet(j, c):
-        pl.semaphore_signal(barrier, inc=1, device_id=at(j)[1], device_id_type=MESH)
-        return c
-
-    lax.fori_loop(1, n, greet, 0)
+    walk(0, n // 2, greet)
+    walk(n // 2, n, greet)
     for load in loads[4:] + loads[1:4]:
         load.start()
 
@@ -106,8 +129,7 @@
         id_send[d] = request[d : d + 1, :]
 
     def send(src, dst, lo, hi, sem, by_owner):
-        def one(j, c):
-            d, where = at(j)
+        def one(j, d, where):
             pltpu.make_async_remote_copy(
                 src_ref=src.at[d if by_owner else j],
                 dst_ref=dst.at[me],
@@ -116,9 +138,8 @@
                 device_id=where,
                 device_id_type=MESH,
             ).start()
-            return c
-
-        lax.fori_loop(max(lo, 1), hi, one, 0)
+
+        walk(lo, hi, one)
 
     others = pl.ds(0, n - 1)
 
@@ -126,7 +147,8 @@
         pltpu.make_async_copy(ref.at[others], ref.at[others], sems.at[sem]).wait()
 
     pl.semaphore_wait(barrier, n - 1)
-    send(id_send, id_recv, 1, n, 0, True)
+    send(id_send, id_recv, 0, n // 2, 0, True)
+    send(id_send, id_recv, n // 2, n, 0, True)
     id_recv[me] = id_send[me]
 
     same = iota((total, total), 0) == iota((total, total), 1)
@@ -139,7 +161,14 @@
     loads[0].wait()
     for g in range(n // group):
         base = g * group
-        source = lax.rem(me + base + iota((256, n), 0) // cap, n)
+        order = base + iota((256, n), 0) // cap
+        x = inner + order // ny
+        if base >= n // 2:
+            x = x - half
+        x = jnp.where(x >= half, x - half, x)
+        y = gy + order % ny
+        source = ((1 - upper if base < n // 2 else upper) * half + x) * ny
+        source = source + jnp.where(y >= ny, y - ny, y)
         expand = jnp.where(source == iota((256, n), 1), 1.0, 0.0).astype(bf16)
         spread = dot(expand, asked)
         place = iota((256, 128), 0) % cap
@@ -157,8 +186,8 @@
         for k in range(group):
             feature_send[base + k] = found[k * cap : (k + 1) * cap, :]
         send(feature_send, feature_recv, base, base + group, 4, False)
-    target_recv[me] = target_send[0]
-    feature_recv[me] = feature_send[0]
+    target_recv[me] = target_send[n // 2]
+    feature_recv[me] = feature_send[n // 2]
 
     for load in loads[1:]:
         load.wait()
@@ -234,22 +263,15 @@
             finish(u + 1, top)
         interest(u, total_weight, context)
 
+    known = joined[...]
+    early = [dot(known, hidden[: 2 * width, :]) for hidden in (click, convert)]
     drain(feature_recv, 5)
-    feature = dot(choose, feature_recv[...].reshape(n * cap, width))
-    joined[:, 2 * width :] = feature.astype(bf16)
-    every = joined[...]
-
-    def tower(hidden, output_ref):
-        act = jnp.maximum(dot(every, hidden[...]), 0.0).astype(bf16)
-        last = output_ref[...].reshape(1, -1)
-        return 1.0 / (1.0 + jnp.exp(-dot(last, act, ((1,), (1,)))))
-
-    rate = tower(click, click_out_ref)
-    both = rate * tower(convert, convert_out_ref)
-    for u in range(users):
-        own = slice(u * per_user, (u + 1) * per_user)
-        rate_ref[u : u + 1, :] = rate[:, own]
-        both_ref[u : u + 1, :] = both[:, own]
+    feature = dot(choose, feature_recv[...].reshape(n * cap, width)).astype(bf16)
+    for i, (hidden, output_ref) in enumerate([(click, click_out_ref), (convert, convert_out_ref)]):
+        act = jnp.maximum(early[i] + dot(feature, hidden[2 * width :, :]), 0.0).astype(bf16)
+        logit = dot(output_ref[...].reshape(1, -1), act, ((1,), (1,)))
+        for u in range(users):
+            logit_ref[i, u : u + 1, :] = logit[:, u * per_user : (u + 1) * per_user]
     drain(id_send, 0)
     drain(target_send, 2)
     drain(feature_send, 4)
@@ -275,14 +297,14 @@
     queries = HEADS * per_user
     vmem = pl.BlockSpec(memory_space=pltpu.VMEM)
     hbm = pl.BlockSpec(memory_space=pl.ANY)
-    out = jax.ShapeDtypeStruct((users, per_user), f32)
+    out = jax.ShapeDtypeStruct((2, users, per_user), f32)
     slab = pltpu.VMEM((n, cap, width), bf16)
     held = [item_table, history, value_weight, click_hidden, convert_hidden]
-    return pl.pallas_call(
+    logits = pl.pallas_call(
         functools.partial(fused_kernel, n, ny, cap),
-        out_shape=(out, out),
+        out_shape=out,
         in_specs=[pl.BlockSpec(memory_space=pltpu.SMEM)] + [vmem] * 3 + [hbm] * 5,
-        out_specs=(vmem, vmem),
+        out_specs=vmem,
         scratch_shapes=[pltpu.VMEM(x.shape, x.dtype) for x in held]
         + [
             pltpu.VMEM((n, 1, 128), f32),
@@ -294,13 +316,15 @@
             slab,
             pltpu.VMEM((2, queries, seq), f32),
             pltpu.VMEM((2, queries, 128), f32),
-            pltpu.VMEM((total, 3 * width), bf16),
+            pltpu.VMEM((total, 2 * width), bf16),
             pltpu.SemaphoreType.DMA((4 + users,)),
             pltpu.SemaphoreType.DMA((6,)),
         ],
         compiler_params=pltpu.CompilerParams(collective_id=0, has_side_effects=True),
         name="esmm",
     )(lengths, candidates, click_output, convert_output, *held)
+    rate = jax.nn.sigmoid(logits[0])
+    return rate, rate * jax.nn.sigmoid(logits[1])
 
 
 def solution(mesh):

time: 32.5 us -> 33.9 us (1.043)
  the two profiles are of different devices: /device:TPU:12 before, /device:TPU:0 now
where the time goes in v2:
time: 33.9 us; the launch traced here: 33.7 us
  Pallas kernels  31.8 us (94%)
  other arithmetic  1.27 us (4%)
  between operations  0.64 us (2%)
    pallas_call x1, Pallas kernels, local(): pl.pallas_call(functools.partial(fused_kernel, n, ny, cap), out_shape=out...  31.8 us
    mul x1, other arithmetic, local(): return (rate, rate * jax.nn.sigmoid(logits[1]))  1.27 us

profile of v2, /device:TPU:0, one launch (start us, length us, event | category | flops | bytes accessed | tf_op | source)
XLA Modules:
  0.0 33.7 jit_solution(17819922529012852162)
XLA Ops:
  0.6 31.8 %esmm.1 = f32[2,4,64]{2,1,0:T(4,128)} custom-call(s32[4]{0:T(128)} %len_ref.1, s32[4,64]{1,0:T(4,128)} %cand_ref.1, bf16[256]{0:T(256)(128)(2,1)} %click_out_ref.1, bf16[256]{0:T(256)(128)(2,1)} %convert_out_ref.1, bf16[4096,512]{1,0:T(8,128)(2,1)} %table_hbm.1, bf16[4,2048,256]{2,1,0:T(8,128)(2,1)} %hist_hbm.1, bf16[256,256]{1,0:T(8,128)(2,1)} %value_hbm.1, ...), custom_call_target="tpu_custom_call" | custom-call | tf_op jit(solution)/shard_map/esmm/pallas_call | solution.py:303
  32.4 1.3 %bitcast_multiply_fusion = (f32[4,64]{1,0:T(4,128)}, f32[4,64]{1,0:T(4,128)}) fusion(f32[2,4,64]{2,1,0:T(4,128)} %esmm.1), kind=kLoop, calls=%fused_computation | loop fusion | flops 1792 | bytes 4096 | tf_op jit(solution)/shard_map/mul | solution.py:327
